TPU v7x, 128 devices: a whole 4x4x4 slice. The times are simulated.
128 devices in a mesh: py: 32 (over z_hi, y, x), px: 4 (over z_lo, core).
Axes of the slice: x: 4, y: 4, z: 4 (z_hi: 2, z_lo: 2; z = z_hi * 2 + z_lo), core: 2. Of those that a mesh axis runs over, the one named last changes fastest.
Arguments:
- source_terms: float32 [2048, 512, 256], P('py', 'px'), may hold values from -6 to 6
- initial_values: float32 [2048, 512, 256], P('py', 'px'), may hold values from -6 to 6
- absorption: float32 [2048, 512, 256], P('py', 'px'), may hold values from 0.1 to 0.9
Outputs:
- improved: float32 [2048, 512, 256], P('py', 'px')
All inputs are finite; a program needn't handle non-finite values.
Results may differ from a plain program's by a relative error of at most 0.00002.
Values sent between devices are 32-bit elements; how exact they have to be, the bound alone decides.
A program may use at most 128 MiB of HBM per device.

v0:
```python
import jax
import jax.numpy as jnp
from jax import lax
from jax.experimental import pallas as pl
from jax.experimental.pallas import tpu as pltpu
from jax.sharding import PartitionSpec as P

MESH = pl.DeviceIdType.MESH
RATIO = 4
INNER = 13
DEPTH = 13
PX = 8
CPX = 16


def coarse_pieces(rows, cols):
    early, late = [], []
    last = rows - 1
    early.append((-1, 0, 1, DEPTH - 1, 0, cols))
    early.append((1, 0, rows - DEPTH, DEPTH - 1, 0, cols))
    for dx in (-1, 1):
        wide = 0 if dx < 0 else cols - 16
        thin = 0 if dx < 0 else cols - 8
        early.append((0, dx, 1, rows - 2, wide, 16))
        early.append((-1, dx, 1, 3, wide, 16))
        early.append((-1, dx, 4, 8, thin, 8))
        early.append((1, dx, last - 3, 3, wide, 16))
        early.append((1, dx, last - 11, 8, thin, 8))
    late.append((-1, 0, 0, 1, 0, cols))
    late.append((1, 0, last, 1, 0, cols))
    for dx in (-1, 1):
        wide = 0 if dx < 0 else cols - 16
        late.append((-1, dx, 0, 1, wide, 16))
        late.append((1, dx, last, 1, wide, 16))
        late.append((0, dx, 0, 1, wide, 16))
        late.append((0, dx, last, 1, wide, 16))
    return early, late


def kernel(ny, nx, source, initial, absorb, out,
           U, V, S, D, W, CL, CW, CA, CB, E, T, LY, LX, KX,
           ld_sem, out_sem, ys, yr, xs, xr, cs, cr):
    J, Y, X = S.shape[0], S.shape[1], S.shape[2]
    CY, CX = Y // RATIO, X // RATIO
    my, mx = lax.axis_index("py"), lax.axis_index("px")

    def device(dy, dx):
        return (lax.rem(my + dy + ny, ny), lax.rem(mx + dx + nx, nx))

    chunks = 4
    step = Y // chunks

    def loads(array, which, ref, padded):
        made = []
        for c in range(chunks):
            for j in range(J):
                if padded:
                    dst = ref.at[j, pl.ds(1 + c * step, step), pl.ds(PX, X), :]
                else:
                    dst = ref.at[j, pl.ds(c * step, step), :, :]
                made.append(pltpu.make_async_copy(
                    array.at[pl.ds(c * step, step), :, pl.ds(j * 128, 128)], dst, ld_sem.at[which, c * J + j]))
        return made

    load_u = loads(initial, 0, U, True)
    load_d = loads(absorb, 1, D, False)
    load_s = loads(source, 2, S, False)
    for copy in load_u + load_d + load_s:
        copy.start()

    around = [(dy, dx) for dy in (-1, 0, 1) for dx in (-1, 0, 1) if (dy, dx) != (0, 0)]
    barrier = pltpu.get_barrier_semaphore()
    for dy, dx in around:
        pl.semaphore_signal(barrier, inc=1, device_id=device(dy, dx), device_id_type=MESH)
    pl.semaphore_wait(barrier, len(around))

    def rows_copies(k, ref):
        return [
            pltpu.make_async_remote_copy(
                src_ref=ref.at[:, 1, pl.ds(PX, X), :], dst_ref=LY.at[k, 1], send_sem=ys.at[k, 1], recv_sem=yr.at[k, 1],
                device_id=device(-1, 0), device_id_type=MESH),
            pltpu.make_async_remote_copy(
                src_ref=ref.at[:, Y, pl.ds(PX, X), :], dst_ref=LY.at[k, 0], send_sem=ys.at[k, 0], recv_sem=yr.at[k, 0],
                device_id=device(1, 0), device_id_type=MESH),
        ]

    def columns_copies(k):
        return [
            pltpu.make_async_remote_copy(
                src_ref=KX.at[k, 1], dst_ref=LX.at[k, 1], send_sem=xs.at[k, 1], recv_sem=xr.at[k, 1],
                device_id=device(0, -1), device_id_type=MESH),
            pltpu.make_async_remote_copy(
                src_ref=KX.at[k, 0], dst_ref=LX.at[k, 0], send_sem=xs.at[k, 0], recv_sem=xr.at[k, 0],
                device_id=device(0, 1), device_id_type=MESH),
        ]

    def start(copies):
        for copy in copies:
            copy.start()

    def received(copies):
        for copy in copies:
            copy.wait_recv()

    def sent(copies):
        for copy in copies:
            copy.wait_send()

    def pack(k, ref):
        def body(y, carry):
            for j in range(J):
                KX[k, 1, j, pl.ds(y, 1), :] = ref[j, y + 1, pl.ds(PX, 1), :]
                KX[k, 0, j, pl.ds(y, 1), :] = ref[j, y + 1, pl.ds(PX + X - 1, 1), :]
            return carry
        lax.fori_loop(0, Y, body, 0)

    def unpack_columns(k, ref):
        def body(y, carry):
            for j in range(J):
                ref[j, y + 1, pl.ds(PX + X, 1), :] = LX[k, 1, j, pl.ds(y, 1), :]
                ref[j, y + 1, pl.ds(PX - 1, 1), :] = LX[k, 0, j, pl.ds(y, 1), :]
            return carry
        lax.fori_loop(0, Y, body, 0)

    def unpack_rows(k, ref):
        for j in range(J):
            ref[j, 0, pl.ds(PX, X), :] = LY[k, 0, j]
            ref[j, Y + 1, pl.ds(PX, X), :] = LY[k, 1, j]

    def neighbours(ref, j, y):
        return (ref[j, y, pl.ds(PX, X), :] + ref[j, y + 2, pl.ds(PX, X), :]
                + (ref[j, y + 1, pl.ds(PX - 1, X), :] + ref[j, y + 1, pl.ds(PX + 1, X), :]))

    def sweep_row(src, dst, y):
        for j in range(J):
            total = S[j, y] + neighbours(src, j, y)
            dst[j, y + 1, pl.ds(PX, X), :] = 0.2 * src[j, y + 1, pl.ds(PX, X), :] + W[j, y] * total

    def inner_rows(src, dst, low, high):
        def body(y, carry):
            sweep_row(src, dst, y)
            return carry
        lax.fori_loop(low, high, body, 0)

    def outer_rows(src, dst):
        def body(i, carry):
            sweep_row(src, dst, i * (Y - 1))
            return carry
        lax.fori_loop(0, 2, body, 0)

    early, late = coarse_pieces(CY, CX)

    def coarse_copies(ref, pieces, base):
        made = []
        for n, (dy, dx, r, nr, c, nc) in enumerate(pieces):
            made.append(pltpu.make_async_remote_copy(
                src_ref=ref.at[:, pl.ds(DEPTH + r, nr), pl.ds(CPX + c, nc), :],
                dst_ref=ref.at[:, pl.ds(DEPTH + r - CY * dy, nr), pl.ds(CPX + c - CX * dx, nc), :],
                send_sem=cs.at[base + n], recv_sem=cr.at[base + n],
                device_id=device(dy, dx), device_id_type=MESH))
        return made

    n_early, n_late = len(early), len(late)
    mass_copies = coarse_copies(CW, early + late, 0)
    load_early = coarse_copies(CL, early, n_early + n_late)
    load_late = coarse_copies(CL, late, 2 * n_early + n_late)

    rows0, rows1, rows2, rows3 = (rows_copies(0, U), rows_copies(1, V), rows_copies(2, U), rows_copies(3, V))
    cols0, cols1, cols2, cols3 = (columns_copies(0), columns_copies(1), columns_copies(2), columns_copies(3))
    for copy in load_u:
        copy.wait()
    start(rows0)
    pack(0, U)
    start(cols0)

    for copy in load_d:
        copy.wait()

    def weight_row(cy, carry):
        for j in range(J):
            total = jnp.zeros((X, 128), jnp.float32)
            for r in range(RATIO):
                mass = D[j, cy * RATIO + r]
                total = total + mass
                whole = 4.0 + mass
                D[j, cy * RATIO + r] = whole
                W[j, cy * RATIO + r] = 0.8 / whole
            T[j] = total
            blocks = (T[j, pl.ds(0, CX, stride=RATIO), :] + T[j, pl.ds(1, CX, stride=RATIO), :]
                      + T[j, pl.ds(2, CX, stride=RATIO), :] + T[j, pl.ds(3, CX, stride=RATIO), :])
            CW[j, DEPTH + cy, pl.ds(CPX, CX), :] = 0.8 / (4.0 + 0.25 * blocks)
        return carry
    lax.fori_loop(0, CY, weight_row, 0)

    for copy in load_s:
        copy.wait()
    received(cols0)
    unpack_columns(0, U)
    inner_rows(U, V, 1, Y - 1)
    received(rows0)
    unpack_rows(0, U)
    outer_rows(U, V)
    start(rows1)
    pack(1, V)
    start(cols1)
    start(mass_copies)

    sent(rows0)
    received(cols1)
    unpack_columns(1, V)
    inner_rows(V, U, 1, Y - 1)
    received(rows1)
    unpack_rows(1, V)
    outer_rows(V, U)
    start(rows2)
    pack(2, U)
    start(cols2)

    def defect_row(cy):
        for j in range(J):
            total = jnp.zeros((X, 128), jnp.float32)
            for r in range(RATIO):
                y = cy * RATIO + r
                total = total + (S[j, y] + neighbours(U, j, y) - D[j, y] * U[j, y + 1, pl.ds(PX, X), :])
            T[j] = total
            blocks = (T[j, pl.ds(0, CX, stride=RATIO), :] + T[j, pl.ds(1, CX, stride=RATIO), :]
                      + T[j, pl.ds(2, CX, stride=RATIO), :] + T[j, pl.ds(3, CX, stride=RATIO), :])
            CL[j, DEPTH + cy, pl.ds(CPX, CX), :] = 0.25 * blocks

    def defect_body(cy, carry):
        defect_row(cy)
        return carry

    def defect_ends(i, carry):
        defect_row(i * (CY - 1))
        return carry

    received(cols2)
    unpack_columns(2, U)
    lax.fori_loop(1, CY - 1, defect_body, 0)
    start(load_early)
    received(rows2)
    unpack_rows(2, U)
    lax.fori_loop(0, 2, defect_ends, 0)
    start(load_late)
    received(mass_copies)
    received(load_early)
    received(load_late)

    wide = CX + 2 * CPX

    def first(y, carry):
        for j in range(J):
            CA[j, y] = CW[j, y] * CL[j, y]
        return carry
    lax.fori_loop(0, CY + 2 * DEPTH, first, 0)
    old, new = CA, CB
    for sweep in range(1, INNER):
        reach = DEPTH - sweep
        x0 = 8 if reach <= 8 else 1
        nx_ = CX + 2 * (CPX - x0)

        def coarse_row(y, carry, old=old, new=new, x0=x0, nx_=nx_):
            for j in range(J):
                total = (CL[j, y, pl.ds(x0, nx_), :] + old[j, y - 1, pl.ds(x0, nx_), :] + old[j, y + 1, pl.ds(x0, nx_), :]
                         + (old[j, y, pl.ds(x0 - 1, nx_), :] + old[j, y, pl.ds(x0 + 1, nx_), :]))
                new[j, y, pl.ds(x0, nx_), :] = 0.2 * old[j, y, pl.ds(x0, nx_), :] + CW[j, y, pl.ds(x0, nx_), :] * total
            return carry
        lax.fori_loop(DEPTH - reach, DEPTH + CY + reach, coarse_row, 0)
        old, new = new, old
    C = old

    def spread(cy):
        for j in range(J):
            cells = C[j, DEPTH + cy, pl.ds(CPX, CX), :]
            for k in range(RATIO):
                E[j, pl.ds(PX + k, CX, stride=RATIO), :] = cells
            E[j, pl.ds(PX - 1, 1), :] = C[j, DEPTH + cy, pl.ds(CPX - 1, 1), :]
            E[j, pl.ds(PX + X, 1), :] = C[j, DEPTH + cy, pl.ds(CPX + CX, 1), :]

    def add_row(y):
        for j in range(J):
            U[j, y] = U[j, y] + E[j]

    sent(rows2)

    def correct(cy, carry):
        spread(cy)
        for r in range(RATIO):
            add_row(1 + cy * RATIO + r)
        return carry

    spread(-1)
    add_row(0)
    lax.fori_loop(0, CY, correct, 0)
    spread(CY)
    add_row(Y + 1)

    sent(rows1)
    outer_rows(U, V)
    start(rows3)
    inner_rows(U, V, 1, Y - 1)
    pack(3, V)
    start(cols3)
    received(cols3)
    unpack_columns(3, V)

    def stores(low, count, sem):
        return [pltpu.make_async_copy(
            U.at[j, pl.ds(1 + low, count), pl.ds(PX, X), :], out.at[pl.ds(low, count), :, pl.ds(j * 128, 128)],
            out_sem.at[sem, j]) for j in range(J)]

    pending = []
    bounds = [1, 16, 32, 48, Y - 1]
    for n in range(4):
        inner_rows(V, U, bounds[n], bounds[n + 1])
        copies = stores(bounds[n], bounds[n + 1] - bounds[n], n)
        start(copies)
        pending += copies
    received(rows3)
    unpack_rows(3, V)
    outer_rows(V, U)
    for n, y in ((4, 0), (5, Y - 1)):
        copies = stores(y, 1, n)
        start(copies)
        pending += copies
    for copy in pending:
        copy.wait()
    sent(rows3)
    for copies in (cols0, cols1, cols2, cols3, mass_copies, load_early, load_late):
        sent(copies)


def solution(mesh):
    ny, nx = mesh.shape["py"], mesh.shape["px"]

    def local(source_terms, initial_values, absorption):
        Y, X, cases = source_terms.shape
        J = cases // 128
        CY, CX = Y // RATIO, X // RATIO
        early, late = coarse_pieces(CY, CX)
        pieces = 2 * (len(early) + len(late))
        f32 = jnp.float32
        fine = pltpu.VMEM((J, Y + 2, X + 2 * PX, 128), f32)
        plain = pltpu.VMEM((J, Y, X, 128), f32)
        coarse = pltpu.VMEM((J, CY + 2 * DEPTH, CX + 2 * CPX, 128), f32)
        dma = pltpu.SemaphoreType.DMA

        def body(*refs):
            kernel(ny, nx, *refs)

        return pl.pallas_call(
            body,
            out_shape=jax.ShapeDtypeStruct((Y, X, cases), f32),
            in_specs=[pl.BlockSpec(memory_space=pl.ANY)] * 3,
            out_specs=pl.BlockSpec(memory_space=pl.ANY),
            scratch_shapes=[
                fine, fine, plain, plain, plain, coarse, coarse, coarse, coarse,
                pltpu.VMEM((J, X + 2 * PX, 128), f32),
                pltpu.VMEM((J, X, 128), f32),
                pltpu.VMEM((4, 2, J, X, 128), f32),
                pltpu.VMEM((4, 2, J, Y, 128), f32),
                pltpu.VMEM((4, 2, J, Y, 128), f32),
                dma((3, 4 * J)), dma((6, J)),
                dma((4, 2)), dma((4, 2)), dma((4, 2)), dma((4, 2)),
                dma((pieces,)), dma((pieces,)),
            ],
            compiler_params=pltpu.CompilerParams(
                collective_id=0, has_side_effects=True, vmem_limit_bytes=67043328),
            name="two_grid",
        )(source_terms, initial_values, absorption)

    spec = P("py", "px", None)
    return jax.shard_map(local, mesh=mesh, in_specs=(spec, spec, spec), out_specs=spec, check_vma=False)
```

profile of v0, /device:TPU:1, one launch (start us, length us, event | category | flops | bytes accessed | tf_op | source)
XLA Modules:
  0.0 109.0 jit_solution(18358546665986442898)
XLA Ops:
  0.0 101.2 %two_grid.1 = f32[64,128,256]{2,1,0:T(8,128)} custom-call(f32[64,128,256]{2,1,0:T(8,128)} %refs_0_.1, f32[64,128,256]{2,1,0:T(8,128)} %refs_1_.1, f32[64,128,256]{2,1,0:T(8,128)} %refs_2_.1), custom_call_target="tpu_custom_call" | custom-call | tf_op jit(solution)/shard_map/two_grid/pallas_call | solution.py:352
  101.2 7.8 %copy.5 = f32[64,128,256]{2,1,0:T(8,128)} copy(f32[64,128,256]{2,1,0:T(8,128)} %two_grid.1) | data formatting | bytes 16777216
where the time goes:
time: 110 us; the launch traced here: 109 us
  Pallas kernels  101 us (92%)
  local copies, waits for them, and re-layouts  7.77 us (7%)
    pallas_call x1, Pallas kernels, local(): pl.pallas_call(body, out_shape=jax.ShapeDtypeStruct((Y, X, cases), f32),...  101 us
    unnamed x1, local copies, waits for them, and re-layouts  7.77 us

commit v1 on v0

v1 whole, which is shorter than its diff:
```python
import jax
import jax.numpy as jnp
from jax import lax
from jax.experimental import pallas as pl
from jax.experimental.pallas import tpu as pltpu
from jax.sharding import PartitionSpec as P

MESH = pl.DeviceIdType.MESH
RATIO = 4
INNER = 13
DEPTH = 6
AGAIN = 7
PX = 8
CPX = 16


def coarse_pieces(depth, rows, cols, part):
    first, last = (0, rows) if part == "all" else (1, rows - 1)
    spans = []
    if part == "late":
        spans += [(-1, 0, 1), (1, rows - 1, 1)]
    else:
        spans += [(-1, first, depth - first), (1, rows - depth, last - (rows - depth))]
    made = [(dy, 0, r, n, 0, cols) for dy, r, n in spans]
    for dx in (-1, 1):
        c = 0 if dx < 0 else cols - 8
        if part == "late":
            made += [(0, dx, 0, 1, c, 8), (0, dx, rows - 1, 1, c, 8), (-1, dx, 0, 1, c, 8), (1, dx, rows - 1, 1, c, 8)]
        else:
            made += [(0, dx, first, last - first, c, 8), (-1, dx, first, depth - 1 - first, c, 8),
                     (1, dx, rows - depth + 1, last - (rows - depth + 1), c, 8)]
    return made


def kernel(ny, nx, source, initial, absorb, D,
           U, V, S, W, CL, CW, CA, CB, CC, E, T, LY, LX, KX,
           ld_sem, ys, yr, xs, xr, cs, cr):
    J, Y, X = S.shape[0], S.shape[1], S.shape[2]
    CY, CX = Y // RATIO, X // RATIO
    my, mx = lax.axis_index("py"), lax.axis_index("px")

    def device(dy, dx):
        return (lax.rem(my + dy + ny, ny), lax.rem(mx + dx + nx, nx))

    chunks = 4
    step = Y // chunks

    def loads(array, which, ref, padded):
        made = []
        for c in range(chunks):
            for j in range(J):
                if padded:
                    dst = ref.at[j, pl.ds(1 + c * step, step), pl.ds(PX, X), :]
                else:
                    dst = ref.at[j, pl.ds(c * step, step), :, :]
                made.append(pltpu.make_async_copy(
                    array.at[pl.ds(c * step, step), :, pl.ds(j * 128, 128)], dst, ld_sem.at[which, c * J + j]))
        return made

    load_u = loads(initial, 0, U, True)
    load_d = loads(absorb, 1, D, False)
    load_s = loads(source, 2, S, False)
    for copy in load_u + load_d + load_s:
        copy.start()

    around = [(dy, dx) for dy in (-1, 0, 1) for dx in (-1, 0, 1) if (dy, dx) != (0, 0)]
    barrier = pltpu.get_barrier_semaphore()
    for dy, dx in around:
        pl.semaphore_signal(barrier, inc=1, device_id=device(dy, dx), device_id_type=MESH)
    with jax.named_scope("barrier"):
        pl.semaphore_wait(barrier, len(around))

    def rows_copies(k, ref):
        return [
            pltpu.make_async_remote_copy(
                src_ref=ref.at[:, 1, pl.ds(PX, X), :], dst_ref=LY.at[k, 1], send_sem=ys.at[k, 1], recv_sem=yr.at[k, 1],
                device_id=device(-1, 0), device_id_type=MESH),
            pltpu.make_async_remote_copy(
                src_ref=ref.at[:, Y, pl.ds(PX, X), :], dst_ref=LY.at[k, 0], send_sem=ys.at[k, 0], recv_sem=yr.at[k, 0],
                device_id=device(1, 0), device_id_type=MESH),
        ]

    def columns_copies(k):
        return [
            pltpu.make_async_remote_copy(
                src_ref=KX.at[k, 1], dst_ref=LX.at[k, 1], send_sem=xs.at[k, 1], recv_sem=xr.at[k, 1],
                device_id=device(0, -1), device_id_type=MESH),
            pltpu.make_async_remote_copy(
                src_ref=KX.at[k, 0], dst_ref=LX.at[k, 0], send_sem=xs.at[k, 0], recv_sem=xr.at[k, 0],
                device_id=device(0, 1), device_id_type=MESH),
        ]

    def start(copies):
        for copy in copies:
            copy.start()

    def received(copies):
        for copy in copies:
            copy.wait_recv()

    def sent(copies):
        for copy in copies:
            copy.wait_send()

    def pack(k, ref):
        def body(y, carry):
            for j in range(J):
                KX[k, 1, j, pl.ds(y, 1), :] = ref[j, y + 1, pl.ds(PX, 1), :]
                KX[k, 0, j, pl.ds(y, 1), :] = ref[j, y + 1, pl.ds(PX + X - 1, 1), :]
            return carry
        lax.fori_loop(0, Y, body, 0)

    def unpack_columns(k, ref):
        def body(y, carry):
            for j in range(J):
                ref[j, y + 1, pl.ds(PX + X, 1), :] = LX[k, 1, j, pl.ds(y, 1), :]
                ref[j, y + 1, pl.ds(PX - 1, 1), :] = LX[k, 0, j, pl.ds(y, 1), :]
            return carry
        lax.fori_loop(0, Y, body, 0)

    def unpack_rows(k, ref):
        for j in range(J):
            ref[j, 0, pl.ds(PX, X), :] = LY[k, 0, j]
            ref[j, Y + 1, pl.ds(PX, X), :] = LY[k, 1, j]

    def neighbours(ref, j, y):
        return (ref[j, y, pl.ds(PX, X), :] + ref[j, y + 2, pl.ds(PX, X), :]
                + (ref[j, y + 1, pl.ds(PX - 1, X), :] + ref[j, y + 1, pl.ds(PX + 1, X), :]))

    def sweep_row(src, dst, y):
        for j in range(J):
            total = S[j, y] + neighbours(src, j, y)
            dst[j, y + 1, pl.ds(PX, X), :] = 0.2 * src[j, y + 1, pl.ds(PX, X), :] + W[j, y] * total

    def inner_rows(src, dst, low, high):
        def body(y, carry):
            sweep_row(src, dst, y)
            return carry
        lax.fori_loop(low, high, body, 0)

    def outer_rows(src, dst):
        def body(i, carry):
            sweep_row(src, dst, i * (Y - 1))
            return carry
        lax.fori_loop(0, 2, body, 0)

    def coarse_copies(ref, depth, part, base):
        made = []
        for n, (dy, dx, r, nr, c, nc) in enumerate(coarse_pieces(depth, CY, CX, part)):
            made.append(pltpu.make_async_remote_copy(
                src_ref=ref.at[:, pl.ds(AGAIN + r, nr), pl.ds(CPX + c, nc), :],
                dst_ref=ref.at[:, pl.ds(AGAIN + r - CY * dy, nr), pl.ds(CPX + c - CX * dx, nc), :],
                send_sem=cs.at[base + n], recv_sem=cr.at[base + n],
                device_id=device(dy, dx), device_id_type=MESH))
        return made

    mass_copies = coarse_copies(CW, DEPTH, "all", 0)
    load_early = coarse_copies(CL, DEPTH, "early", 8)
    load_late = coarse_copies(CL, DEPTH, "late", 16)
    value_copies = coarse_copies(CC, AGAIN, "all", 26)

    rows0, rows1, rows2, rows3 = (rows_copies(0, U), rows_copies(1, V), rows_copies(2, U), rows_copies(3, V))
    cols0, cols1, cols2, cols3 = (columns_copies(0), columns_copies(1), columns_copies(2), columns_copies(3))
    with jax.named_scope("wait_u"):
        for copy in load_u:
            copy.wait()
    with jax.named_scope("pack0"):
        start(rows0)
        pack(0, U)
        start(cols0)

    with jax.named_scope("wait_d"):
        for copy in load_d:
            copy.wait()

    def weight_row(cy, carry):
        for j in range(J):
            total = jnp.zeros((X, 128), jnp.float32)
            for r in range(RATIO):
                mass = D[j, cy * RATIO + r]
                total = total + mass
                whole = 4.0 + mass
                D[j, cy * RATIO + r] = whole
                W[j, cy * RATIO + r] = 0.8 / whole
            T[j] = total
            blocks = (T[j, pl.ds(0, CX, stride=RATIO), :] + T[j, pl.ds(1, CX, stride=RATIO), :]
                      + T[j, pl.ds(2, CX, stride=RATIO), :] + T[j, pl.ds(3, CX, stride=RATIO), :])
            CW[j, AGAIN + cy, pl.ds(CPX, CX), :] = 0.8 / (4.0 + 0.25 * blocks)
        return carry
    with jax.named_scope("weights"):
        lax.fori_loop(0, CY, weight_row, 0)
        start(mass_copies)

    with jax.named_scope("wait_s_x0"):
        for copy in load_s:
            copy.wait()
        received(cols0)
    with jax.named_scope("sweep1"):
        unpack_columns(0, U)
        inner_rows(U, V, 1, Y - 1)
    with jax.named_scope("wait_y0"):
        received(rows0)
    with jax.named_scope("outer1"):
        unpack_rows(0, U)
        outer_rows(U, V)
        start(rows1)
        pack(1, V)
        start(cols1)

    with jax.named_scope("wait_x1"):
        sent(rows0)
        received(cols1)
    with jax.named_scope("sweep2"):
        unpack_columns(1, V)
        inner_rows(V, U, 1, Y - 1)
    with jax.named_scope("wait_y1"):
        received(rows1)
    with jax.named_scope("outer2"):
        unpack_rows(1, V)
        outer_rows(V, U)
        start(rows2)
        pack(2, U)
        start(cols2)

    def defect_row(cy):
        for j in range(J):
            total = jnp.zeros((X, 128), jnp.float32)
            for r in range(RATIO):
                y = cy * RATIO + r
                total = total + (S[j, y] + neighbours(U, j, y) - D[j, y] * U[j, y + 1, pl.ds(PX, X), :])
            T[j] = total
            blocks = (T[j, pl.ds(0, CX, stride=RATIO), :] + T[j, pl.ds(1, CX, stride=RATIO), :]
                      + T[j, pl.ds(2, CX, stride=RATIO), :] + T[j, pl.ds(3, CX, stride=RATIO), :])
            CL[j, AGAIN + cy, pl.ds(CPX, CX), :] = 0.25 * blocks

    def defect_body(cy, carry):
        defect_row(cy)
        return carry

    def defect_ends(i, carry):
        defect_row(i * (CY - 1))
        return carry

    with jax.named_scope("wait_x2"):
        received(cols2)
    with jax.named_scope("defect"):
        unpack_columns(2, U)
        lax.fori_loop(1, CY - 1, defect_body, 0)
        start(load_early)
    with jax.named_scope("wait_y2"):
        received(rows2)
    with jax.named_scope("defect_ends"):
        unpack_rows(2, U)
        lax.fori_loop(0, 2, defect_ends, 0)
        start(load_late)
    with jax.named_scope("wait_mass"):
        received(mass_copies)
    with jax.named_scope("wait_load"):
        received(load_early)
        received(load_late)

    def first(y, carry):
        for j in range(J):
            CA[j, y] = CW[j, y] * CL[j, y]
        return carry

    def coarse_sweep(old, new, reach):
        x0 = CPX - 8 if reach > 0 else CPX
        wide = CX + 2 * (CPX - x0)

        def coarse_row(y, carry):
            for j in range(J):
                total = (CL[j, y, pl.ds(x0, wide), :] + old[j, y - 1, pl.ds(x0, wide), :] + old[j, y + 1, pl.ds(x0, wide), :]
                         + (old[j, y, pl.ds(x0 - 1, wide), :] + old[j, y, pl.ds(x0 + 1, wide), :]))
                new[j, y, pl.ds(x0, wide), :] = 0.2 * old[j, y, pl.ds(x0, wide), :] + CW[j, y, pl.ds(x0, wide), :] * total
            return carry
        lax.fori_loop(AGAIN - reach, AGAIN + CY + reach, coarse_row, 0)

    with jax.named_scope("coarse1"):
        lax.fori_loop(AGAIN - DEPTH, AGAIN + CY + DEPTH, first, 0)
        old, new = CA, CB
        for reach in range(DEPTH - 1, -1, -1):
            coarse_sweep(old, CC if reach == 0 else new, reach)
            old, new = new, old
        start(value_copies)
    with jax.named_scope("wait_value"):
        received(value_copies)
    with jax.named_scope("coarse2"):
        old, new = CC, CA
        for reach in range(AGAIN - 1, 0, -1):
            coarse_sweep(old, new, reach)
            old, new = new, (CB if new is CA else CA)
        C = old

    def spread(cy):
        for j in range(J):
            cells = C[j, AGAIN + cy, pl.ds(CPX, CX), :]
            for k in range(RATIO):
                E[j, pl.ds(PX + k, CX, stride=RATIO), :] = cells
            E[j, pl.ds(PX - 1, 1), :] = C[j, AGAIN + cy, pl.ds(CPX - 1, 1), :]
            E[j, pl.ds(PX + X, 1), :] = C[j, AGAIN + cy, pl.ds(CPX + CX, 1), :]

    def add_row(y):
        for j in range(J):
            U[j, y] = U[j, y] + E[j]

    sent(rows2)

    def correct(cy, carry):
        spread(cy)
        for r in range(RATIO):
            add_row(1 + cy * RATIO + r)
        return carry

    spread(-1)
    add_row(0)
    with jax.named_scope("correct"):
        lax.fori_loop(0, CY, correct, 0)
        spread(CY)
        add_row(Y + 1)

    sent(rows1)
    with jax.named_scope("sweep3"):
        outer_rows(U, V)
        start(rows3)
        inner_rows(U, V, 1, Y - 1)
        pack(3, V)
        start(cols3)
    with jax.named_scope("wait_x3"):
        received(cols3)
    unpack_columns(3, V)

    def last_row(y, carry):
        for j in range(J):
            total = S[j, y] + neighbours(V, j, y)
            D[j, y] = 0.2 * V[j, y + 1, pl.ds(PX, X), :] + W[j, y] * total
        return carry

    with jax.named_scope("sweep4"):
        lax.fori_loop(1, Y - 1, last_row, 0)
    with jax.named_scope("wait_y3"):
        received(rows3)
    with jax.named_scope("outer4"):
        unpack_rows(3, V)
        lax.fori_loop(0, 2, lambda i, carry: last_row(i * (Y - 1), carry), 0)
    sent(rows3)
    for copies in (cols0, cols1, cols2, cols3, mass_copies, load_early, load_late, value_copies):
        sent(copies)


def store(held, out, sems):
    J, Y, X = held.shape[0], held.shape[1], held.shape[2]
    copies = []
    for n in range(4):
        for j in range(J):
            rows = pl.ds(n * Y // 4, Y // 4)
            copies.append(pltpu.make_async_copy(held.at[j, rows], out.at[rows, :, pl.ds(j * 128, 128)], sems.at[n, j]))
    for copy in copies:
        copy.start()
    for copy in copies:
        copy.wait()


def solution(mesh):
    ny, nx = mesh.shape["py"], mesh.shape["px"]

    def local(source_terms, initial_values, absorption):
        Y, X, cases = source_terms.shape
        J = cases // 128
        CY, CX = Y // RATIO, X // RATIO
        f32 = jnp.float32
        fine = pltpu.VMEM((J, Y + 2, X + 2 * PX, 128), f32)
        plain = pltpu.VMEM((J, Y, X, 128), f32)
        coarse = pltpu.VMEM((J, CY + 2 * AGAIN, CX + 2 * CPX, 128), f32)
        dma = pltpu.SemaphoreType.DMA

        def body(*refs):
            kernel(ny, nx, *refs)

        held = pl.pallas_call(
            body,
            out_shape=plain,
            in_specs=[pl.BlockSpec(memory_space=pl.ANY)] * 3,
            out_specs=pl.BlockSpec(memory_space=pltpu.VMEM),
            scratch_shapes=[
                fine, fine, plain, plain, coarse, coarse, coarse, coarse, coarse,
                pltpu.VMEM((J, X + 2 * PX, 128), f32),
                pltpu.VMEM((J, X, 128), f32),
                pltpu.VMEM((4, 2, J, X, 128), f32),
                pltpu.VMEM((4, 2, J, Y, 128), f32),
                pltpu.VMEM((4, 2, J, Y, 128), f32),
                dma((3, 4 * J)),
                dma((4, 2)), dma((4, 2)), dma((4, 2)), dma((4, 2)),
                dma((34,)), dma((34,)),
            ],
            compiler_params=pltpu.CompilerParams(
                collective_id=0, has_side_effects=True, vmem_limit_bytes=50 * 1024 * 1024),
            name="two_grid",
        )(source_terms, initial_values, absorption)
        return pl.pallas_call(
            store,
            out_shape=jax.ShapeDtypeStruct((Y, X, cases), f32),
            in_specs=[pl.BlockSpec(memory_space=pltpu.VMEM)],
            out_specs=pl.BlockSpec(memory_space=pl.ANY),
            scratch_shapes=[dma((4, J))],
            compiler_params=pltpu.CompilerParams(vmem_limit_bytes=1024 * 1024),
            name="store",
        )(pltpu.with_memory_space_constraint(held, pltpu.VMEM))

    spec = P("py", "px", None)
    return jax.shard_map(local, mesh=mesh, in_specs=(spec, spec, spec), out_specs=spec, check_vma=False)
```

time: 110 us -> 86.4 us (0.79)
  Pallas kernels: 101 us -> 86.3 us
  local copies, waits for them, and re-layouts: 7.77 us -> 0 us
    pallas_call x1 -> x2, Pallas kernels: 101 us -> 86.3 us  [the longest x1 82.9 us: local(): pl.pallas_call(body, out_shape=plain, in_specs=[pl.BlockSpec(memory_space...]
    unnamed x1 -> x0, local copies, waits for them, and re-layouts: 7.77 us -> none
where the time goes in v1:
time: 86.4 us; the launch traced here: 86.3 us
  Pallas kernels  86.3 us (100%)
    pallas_call x1, Pallas kernels, local(): pl.pallas_call(body, out_shape=plain, in_specs=[pl.BlockSpec(memory_space...  82.9 us
    pallas_call x1, Pallas kernels, local(): pl.pallas_call(store, out_shape=jax.ShapeDtypeStruct((Y, X, cases), f32),...  3.37 us

profile of v1, /device:TPU:1, one launch (start us, length us, event | category | flops | bytes accessed | tf_op | source)
XLA Modules:
  0.0 86.3 jit_solution(3790288001420085252)
XLA Ops:
  0.0 82.9 %two_grid.1.held = f32[2,64,128,128]{3,2,1,0:T(8,128)S(1)} custom-call(f32[64,128,256]{2,1,0:T(8,128)} %refs_0_.1, f32[64,128,256]{2,1,0:T(8,128)} %refs_1_.1, f32[64,128,256]{2,1,0:T(8,128)} %refs_2_.1), custom_call_target="tpu_custom_call" | custom-call | tf_op jit(solution)/shard_map/two_grid/pallas_call | solution.py:380
  82.9 3.4 %store.1 = f32[64,128,256]{2,1,0:T(8,128)} custom-call(f32[2,64,128,128]{3,2,1,0:T(8,128)S(1)} %two_grid.1.held), custom_call_target="tpu_custom_call" | custom-call | tf_op jit(solution)/shard_map/store/pallas_call | solution.py:400

commit v2 on v1

v2 whole, which is shorter than its diff:
```python
import jax
import jax.numpy as jnp
from jax import lax
from jax.experimental import pallas as pl
from jax.experimental.pallas import tpu as pltpu
from jax.sharding import PartitionSpec as P

MESH = pl.DeviceIdType.MESH
RATIO = 4
INNER = 13
DEPTH = 6
AGAIN = 7
PX = 8
CPX = 16


CORNERS = [(-1, -1), (-1, 1), (1, -1), (1, 1)]


def corner_cells(depth, rows, cols, dy, dx):
    cells, place = [], 0
    for k in range(1, depth):
        n = depth - k
        here, there = (k - 1, rows + k - 1) if dy < 0 else (rows - k, -k)
        cells.append((here, there, 0, cols, n, place) if dx < 0 else (here, there, cols - n, -n, n, place))
        place += n
    return cells


def kernel(ny, nx, source, initial, absorb, D,
           U, V, S, W, CL, CW, CA, CB, CC, E, T, LY, LX, KX, KC, LC,
           ld_sem, ys, yr, xs, xr, cs, cr):
    J, Y, X = S.shape[0], S.shape[1], S.shape[2]
    CY, CX = Y // RATIO, X // RATIO
    my, mx = lax.axis_index("py"), lax.axis_index("px")

    def device(dy, dx):
        return (lax.rem(my + dy + ny, ny), lax.rem(mx + dx + nx, nx))

    def loads(array, ref, padded, spans, base):
        made = []
        for low, count in spans:
            for j in range(J):
                if padded:
                    dst = ref.at[j, pl.ds(1 + low, count), pl.ds(PX, X), :]
                else:
                    dst = ref.at[j, pl.ds(low, count), :, :]
                made.append(pltpu.make_async_copy(
                    array.at[pl.ds(low, count), :, pl.ds(j * 128, 128)], dst, ld_sem.at[base + len(made)]))
        return made

    quarters = [(n * Y // 4, Y // 4) for n in range(4)]
    load_ends = loads(initial, U, True, [(0, 1), (Y - 1, 1)], 0)
    load_u = loads(initial, U, True, [(1, 15), (16, 16), (32, 16), (48, Y - 49)], 2 * J)
    load_d = loads(absorb, D, False, quarters, 6 * J)
    load_s = loads(source, S, False, quarters, 10 * J)
    for copy in load_ends + load_u + load_d + load_s:
        copy.start()

    around = [(dy, dx) for dy in (-1, 0, 1) for dx in (-1, 0, 1) if (dy, dx) != (0, 0)]
    barrier = pltpu.get_barrier_semaphore()
    for dy, dx in around:
        pl.semaphore_signal(barrier, inc=1, device_id=device(dy, dx), device_id_type=MESH)
    with jax.named_scope("barrier"):
        pl.semaphore_wait(barrier, len(around))

    def rows_copies(k, ref):
        return [
            pltpu.make_async_remote_copy(
                src_ref=ref.at[:, 1, pl.ds(PX, X), :], dst_ref=LY.at[k, 1], send_sem=ys.at[k, 1], recv_sem=yr.at[k, 1],
                device_id=device(-1, 0), device_id_type=MESH),
            pltpu.make_async_remote_copy(
                src_ref=ref.at[:, Y, pl.ds(PX, X), :], dst_ref=LY.at[k, 0], send_sem=ys.at[k, 0], recv_sem=yr.at[k, 0],
                device_id=device(1, 0), device_id_type=MESH),
        ]

    def columns_copies(k):
        return [
            pltpu.make_async_remote_copy(
                src_ref=KX.at[k, 1], dst_ref=LX.at[k, 1], send_sem=xs.at[k, 1], recv_sem=xr.at[k, 1],
                device_id=device(0, -1), device_id_type=MESH),
            pltpu.make_async_remote_copy(
                src_ref=KX.at[k, 0], dst_ref=LX.at[k, 0], send_sem=xs.at[k, 0], recv_sem=xr.at[k, 0],
                device_id=device(0, 1), device_id_type=MESH),
        ]

    def start(copies):
        for copy in copies:
            copy.start()

    def received(copies):
        for copy in copies:
            copy.wait_recv()

    def sent(copies):
        for copy in copies:
            copy.wait_send()

    def pack(k, ref):
        def body(y, carry):
            for j in range(J):
                KX[k, 1, j, pl.ds(y, 1), :] = ref[j, y + 1, pl.ds(PX, 1), :]
                KX[k, 0, j, pl.ds(y, 1), :] = ref[j, y + 1, pl.ds(PX + X - 1, 1), :]
            return carry
        lax.fori_loop(0, Y, body, 0)

    def unpack_columns(k, ref):
        def body(y, carry):
            for j in range(J):
                ref[j, y + 1, pl.ds(PX + X, 1), :] = LX[k, 1, j, pl.ds(y, 1), :]
                ref[j, y + 1, pl.ds(PX - 1, 1), :] = LX[k, 0, j, pl.ds(y, 1), :]
            return carry
        lax.fori_loop(0, Y, body, 0)

    def unpack_rows(k, ref):
        for j in range(J):
            ref[j, 0, pl.ds(PX, X), :] = LY[k, 0, j]
            ref[j, Y + 1, pl.ds(PX, X), :] = LY[k, 1, j]

    def residual_rows(src, j, y, n, x, w):
        r = [src[j, y + k, pl.ds(PX + x, w), :] for k in range(n + 2)]
        for k in range(n):
            beside = src[j, y + k + 1, pl.ds(PX + x - 1, w), :] + src[j, y + k + 1, pl.ds(PX + x + 1, w), :]
            yield k, r[k + 1], S[j, y + k, pl.ds(x, w), :] + (r[k] + r[k + 2] + beside)

    def relax(src, put, y, n, columns):
        for j in range(J):
            for x, w in columns:
                for k, old, total in residual_rows(src, j, y, n, x, w):
                    put(j, y + k, x, w, 0.2 * old + W[j, y + k, pl.ds(x, w), :] * total)

    def into(ref):
        def put(j, y, x, w, value):
            ref[j, y + 1, pl.ds(PX + x, w), :] = value
        return put

    def into_result(j, y, x, w, value):
        D[j, y, pl.ds(x, w), :] = value

    middle_columns = [(x, min(32, X - 8 - x)) for x in range(8, X - 8, 32)]
    edge_columns = [(0, 8), (X - 8, 8)]
    all_columns = [(x, 32) for x in range(0, X, 32)]

    def inner(src, put, columns):
        def body(i, carry):
            relax(src, put, 2 + 4 * i, 4, columns)
            return carry
        lax.fori_loop(0, (Y - 4) // 4, body, 0)

    def outer(src, put):
        def body(i, carry):
            relax(src, put, i * (Y - 2), 2, all_columns)
            return carry
        lax.fori_loop(0, 2, body, 0)

    def coarse_copies(ref, pieces, base):
        made = []
        for n, (dy, dx, r, nr, c, nc) in enumerate(pieces):
            made.append(pltpu.make_async_remote_copy(
                src_ref=ref.at[:, pl.ds(AGAIN + r, nr), pl.ds(CPX + c, nc), :],
                dst_ref=ref.at[:, pl.ds(AGAIN + r - CY * dy, nr), pl.ds(CPX + c - CX * dx, nc), :],
                send_sem=cs.at[base + n], recv_sem=cr.at[base + n],
                device_id=device(dy, dx), device_id_type=MESH))
        return made

    def corner_copies(which, cells, base):
        return [pltpu.make_async_remote_copy(
            src_ref=KC.at[which, n, :, pl.ds(0, cells), :], dst_ref=LC.at[which, n, :, pl.ds(0, cells), :],
            send_sem=cs.at[base + n], recv_sem=cr.at[base + n],
            device_id=device(dy, dx), device_id_type=MESH) for n, (dy, dx) in enumerate(CORNERS)]

    def pack_corners(which, ref, depth):
        for n, (dy, dx) in enumerate(CORNERS):
            for here, _, c, _, count, place in corner_cells(depth, CY, CX, dy, dx):
                for j in range(J):
                    KC[which, n, j, pl.ds(place, count), :] = ref[j, AGAIN + here, pl.ds(CPX + c, count), :]

    def unpack_corners(which, ref, depth):
        for n, (dy, dx) in enumerate(CORNERS):
            for _, there, _, c, count, place in corner_cells(depth, CY, CX, dy, dx):
                for j in range(J):
                    ref[j, AGAIN + there, pl.ds(CPX + c, count), :] = LC[which, n, j, pl.ds(place, count), :]

    def sides(first, last):
        return [(0, -1, first, last - first, 0, 8), (0, 1, first, last - first, CX - 8, 8)]

    half = DEPTH // 2
    mass_near = coarse_copies(CW, [(-1, 0, 0, half, 0, CX), (1, 0, CY - half, half, 0, CX)], 0)
    mass_far = coarse_copies(
        CW, [(-1, 0, half, DEPTH - half, 0, CX), (1, 0, CY - DEPTH, DEPTH - half, 0, CX)] + sides(0, CY), 2)
    mass_corners = corner_copies(0, 16, 6)
    load_early = coarse_copies(CL, [(-1, 0, 1, DEPTH - 1, 0, CX), (1, 0, CY - DEPTH, DEPTH - 1, 0, CX)], 10)
    load_late = coarse_copies(CL, [(-1, 0, 0, 1, 0, CX), (1, 0, CY - 1, 1, 0, CX)] + sides(0, CY), 12)
    load_corners = corner_copies(1, 16, 16)
    value_copies = coarse_copies(CC, [(-1, 0, 0, AGAIN, 0, CX), (1, 0, CY - AGAIN, AGAIN, 0, CX)] + sides(0, CY), 20)
    value_corners = corner_copies(2, 24, 24)

    rows0, rows1, rows2, rows3 = (rows_copies(0, U), rows_copies(1, V), rows_copies(2, U), rows_copies(3, V))
    cols0, cols1, cols2, cols3 = (columns_copies(0), columns_copies(1), columns_copies(2), columns_copies(3))
    with jax.named_scope("wait_ends"):
        for copy in load_ends:
            copy.wait()
        start(rows0)
    with jax.named_scope("wait_u"):
        for copy in load_u:
            copy.wait()
    with jax.named_scope("pack0"):
        pack(0, U)
        start(cols0)

    with jax.named_scope("wait_d"):
        for copy in load_d:
            copy.wait()

    def fold(ref, j):
        return (ref[j, pl.ds(0, CX, stride=RATIO), :] + ref[j, pl.ds(1, CX, stride=RATIO), :]
                + ref[j, pl.ds(2, CX, stride=RATIO), :] + ref[j, pl.ds(3, CX, stride=RATIO), :])

    def weight_row(cy, carry):
        for j in range(J):
            total = jnp.zeros((X, 128), jnp.float32)
            for r in range(RATIO):
                mass = D[j, cy * RATIO + r]
                total = total + mass
                whole = 4.0 + mass
                D[j, cy * RATIO + r] = whole
                W[j, cy * RATIO + r] = 0.8 / whole
            T[j, 0] = total
            CW[j, AGAIN + cy, pl.ds(CPX, CX), :] = 0.8 / (4.0 + 0.25 * fold(T.at[:, 0], j))
        return carry
    with jax.named_scope("weights"):
        lax.fori_loop(0, CY, weight_row, 0)
        start(mass_near)

    with jax.named_scope("wait_s"):
        for copy in load_s:
            copy.wait()
    with jax.named_scope("middle1"):
        inner(U, into(V), middle_columns)
    with jax.named_scope("wait_x0"):
        received(cols0)
    with jax.named_scope("edges1"):
        unpack_columns(0, U)
        inner(U, into(V), edge_columns)
    with jax.named_scope("wait_y0"):
        received(rows0)
    with jax.named_scope("outer1"):
        unpack_rows(0, U)
        outer(U, into(V))
        start(rows1)
        pack(1, V)
        start(cols1)
        start(mass_far)
        pack_corners(0, CW, DEPTH)
        start(mass_corners)

    sent(rows0)
    with jax.named_scope("middle2"):
        inner(V, into(U), middle_columns)
    with jax.named_scope("wait_x1"):
        received(cols1)
    with jax.named_scope("edges2"):
        unpack_columns(1, V)
        inner(V, into(U), edge_columns)
    with jax.named_scope("wait_y1"):
        received(rows1)
    with jax.named_scope("outer2"):
        unpack_rows(1, V)
        outer(V, into(U))
        start(rows2)
        pack(2, U)
        start(cols2)

    def defect(cy, columns):
        for j in range(J):
            for x, w in columns:
                total = None
                for k, old, around in residual_rows(U, j, cy * RATIO, RATIO, x, w):
                    term = around - D[j, cy * RATIO + k, pl.ds(x, w), :] * old
                    total = term if total is None else total + term
                T[j, cy, pl.ds(x, w), :] = total

    def coarse_load(cy):
        for j in range(J):
            CL[j, AGAIN + cy, pl.ds(CPX, CX), :] = 0.25 * fold(T.at[:, cy], j)

    def defect_middle(cy, carry):
        defect(cy, middle_columns)
        return carry

    def defect_edges(cy, carry):
        defect(cy, edge_columns)
        coarse_load(cy)
        return carry

    def defect_ends(i, carry):
        defect(i * (CY - 1), all_columns)
        coarse_load(i * (CY - 1))
        return carry

    with jax.named_scope("defect_middle"):
        lax.fori_loop(1, CY - 1, defect_middle, 0)
    with jax.named_scope("wait_x2"):
        received(cols2)
    with jax.named_scope("defect_edges"):
        unpack_columns(2, U)
        lax.fori_loop(1, CY - 1, defect_edges, 0)
        start(load_early)
    with jax.named_scope("wait_y2"):
        received(rows2)
    with jax.named_scope("defect_ends"):
        unpack_rows(2, U)
        lax.fori_loop(0, 2, defect_ends, 0)
        start(load_late)
        pack_corners(1, CL, DEPTH)
        start(load_corners)
    with jax.named_scope("wait_mass"):
        received(mass_near + mass_far + mass_corners)
        unpack_corners(0, CW, DEPTH)
    with jax.named_scope("wait_load"):
        received(load_early + load_late + load_corners)
        unpack_corners(1, CL, DEPTH)

    def first(y, carry):
        for j in range(J):
            CA[j, y] = CW[j, y] * CL[j, y]
        return carry

    def coarse_sweep(old, new, reach):
        x0 = CPX - 8 if reach > 0 else CPX
        wide = CX + 2 * (CPX - x0)

        n = 4 if (CY + 2 * reach) % 4 == 0 else 2
        half = wide // 2

        def coarse_rows(i, carry):
            y = AGAIN - reach + n * i
            for j in range(J):
                for x in (x0, x0 + half):
                    r = [old[j, y - 1 + k, pl.ds(x, half), :] for k in range(n + 2)]
                    for k in range(n):
                        beside = old[j, y + k, pl.ds(x - 1, half), :] + old[j, y + k, pl.ds(x + 1, half), :]
                        total = CL[j, y + k, pl.ds(x, half), :] + (r[k] + r[k + 2] + beside)
                        new[j, y + k, pl.ds(x, half), :] = 0.2 * r[k + 1] + CW[j, y + k, pl.ds(x, half), :] * total
            return carry
        lax.fori_loop(0, (CY + 2 * reach) // n, coarse_rows, 0)

    with jax.named_scope("coarse1"):
        lax.fori_loop(AGAIN - DEPTH, AGAIN + CY + DEPTH, first, 0)
        old, new = CA, CB
        for reach in range(DEPTH - 1, -1, -1):
            coarse_sweep(old, CC if reach == 0 else new, reach)
            old, new = new, old
        start(value_copies)
        pack_corners(2, CC, AGAIN)
        start(value_corners)
    with jax.named_scope("wait_value"):
        received(value_copies + value_corners)
        unpack_corners(2, CC, AGAIN)
    with jax.named_scope("coarse2"):
        old, new = CC, CA
        for reach in range(AGAIN - 1, 0, -1):
            coarse_sweep(old, new, reach)
            old, new = new, (CB if new is CA else CA)
        C = old

    def spread(cy):
        for j in range(J):
            cells = C[j, AGAIN + cy, pl.ds(CPX, CX), :]
            for k in range(RATIO):
                E[j, pl.ds(PX + k, CX, stride=RATIO), :] = cells
            E[j, pl.ds(PX - 1, 1), :] = C[j, AGAIN + cy, pl.ds(CPX - 1, 1), :]
            E[j, pl.ds(PX + X, 1), :] = C[j, AGAIN + cy, pl.ds(CPX + CX, 1), :]

    def add_row(y):
        for j in range(J):
            U[j, y] = U[j, y] + E[j]

    sent(rows2)

    def correct(cy, carry):
        spread(cy)
        for r in range(RATIO):
            add_row(1 + cy * RATIO + r)
        return carry

    spread(-1)
    add_row(0)
    with jax.named_scope("correct"):
        lax.fori_loop(0, CY, correct, 0)
        spread(CY)
        add_row(Y + 1)

    sent(rows1)
    with jax.named_scope("outer3"):
        outer(U, into(V))
        start(rows3)
    with jax.named_scope("sweep3"):
        inner(U, into(V), edge_columns)
        pack(3, V)
        start(cols3)
        inner(U, into(V), middle_columns)
    with jax.named_scope("middle4"):
        inner(V, into_result, middle_columns)
    with jax.named_scope("wait_x3"):
        received(cols3)
    with jax.named_scope("edges4"):
        unpack_columns(3, V)
        inner(V, into_result, edge_columns)
    with jax.named_scope("wait_y3"):
        received(rows3)
    with jax.named_scope("outer4"):
        unpack_rows(3, V)
        outer(V, into_result)
    sent(rows3)
    for copies in (cols0, cols1, cols2, cols3, mass_near, mass_far, mass_corners, load_early, load_late, load_corners,
                   value_copies, value_corners):
        sent(copies)


def store(held, out, sems):
    J, Y, X = held.shape[0], held.shape[1], held.shape[2]
    copies = []
    for n in range(4):
        for j in range(J):
            rows = pl.ds(n * Y // 4, Y // 4)
            copies.append(pltpu.make_async_copy(held.at[j, rows], out.at[rows, :, pl.ds(j * 128, 128)], sems.at[n, j]))
    for copy in copies:
        copy.start()
    for copy in copies:
        copy.wait()


def solution(mesh):
    ny, nx = mesh.shape["py"], mesh.shape["px"]

    def local(source_terms, initial_values, absorption):
        Y, X, cases = source_terms.shape
        J = cases // 128
        CY, CX = Y // RATIO, X // RATIO
        f32 = jnp.float32
        fine = pltpu.VMEM((J, Y + 2, X + 2 * PX, 128), f32)
        plain = pltpu.VMEM((J, Y, X, 128), f32)
        coarse = pltpu.VMEM((J, CY + 2 * AGAIN, CX + 2 * CPX, 128), f32)
        dma = pltpu.SemaphoreType.DMA

        def body(*refs):
            kernel(ny, nx, *refs)

        held = pl.pallas_call(
            body,
            out_shape=plain,
            in_specs=[pl.BlockSpec(memory_space=pl.ANY)] * 3,
            out_specs=pl.BlockSpec(memory_space=pltpu.VMEM),
            scratch_shapes=[
                fine, fine, plain, plain, coarse, coarse, coarse, coarse, coarse,
                pltpu.VMEM((J, X + 2 * PX, 128), f32),
                pltpu.VMEM((J, CY, X, 128), f32),
                pltpu.VMEM((4, 2, J, X, 128), f32),
                pltpu.VMEM((4, 2, J, Y, 128), f32),
                pltpu.VMEM((4, 2, J, Y, 128), f32),
                pltpu.VMEM((3, 4, J, 24, 128), f32),
                pltpu.VMEM((3, 4, J, 24, 128), f32),
                dma((14 * J,)),
                dma((4, 2)), dma((4, 2)), dma((4, 2)), dma((4, 2)),
                dma((28,)), dma((28,)),
            ],
            compiler_params=pltpu.CompilerParams(
                collective_id=0, has_side_effects=True, vmem_limit_bytes=52 * 1024 * 1024),
            name="two_grid",
        )(source_terms, initial_values, absorption)
        return pl.pallas_call(
            store,
            out_shape=jax.ShapeDtypeStruct((Y, X, cases), f32),
            in_specs=[pl.BlockSpec(memory_space=pltpu.VMEM)],
            out_specs=pl.BlockSpec(memory_space=pl.ANY),
            scratch_shapes=[dma((4, J))],
            compiler_params=pltpu.CompilerParams(vmem_limit_bytes=1024 * 1024),
            name="store",
        )(pltpu.with_memory_space_constraint(held, pltpu.VMEM))

    spec = P("py", "px", None)
    return jax.shard_map(local, mesh=mesh, in_specs=(spec, spec, spec), out_specs=spec, check_vma=False)
```

time: 86.4 us -> 72 us (0.83)
  Pallas kernels: 86.3 us -> 71.9 us
    pallas_call x1, Pallas kernels: 82.9 us -> 68.5 us  [local(): pl.pallas_call(body, out_shape=plain, in_specs=[pl.BlockSpec(memory_space...]
where the time goes in v2:
time: 72 us; the launch traced here: 71.9 us
  Pallas kernels  71.9 us (100%)
    pallas_call x1, Pallas kernels, local(): pl.pallas_call(body, out_shape=plain, in_specs=[pl.BlockSpec(memory_space...  68.5 us
    pallas_call x1, Pallas kernels, local(): pl.pallas_call(store, out_shape=jax.ShapeDtypeStruct((Y, X, cases), f32),...  3.37 us

profile of v2, /device:TPU:1, one launch (start us, length us, event | category | flops | bytes accessed | tf_op | source)
XLA Modules:
  0.0 71.9 jit_solution(11116721177208929420)
XLA Ops:
  0.0 68.5 %two_grid.1.held = f32[2,64,128,128]{3,2,1,0:T(8,128)S(1)} custom-call(f32[64,128,256]{2,1,0:T(8,128)} %refs_0_.1, f32[64,128,256]{2,1,0:T(8,128)} %refs_1_.1, f32[64,128,256]{2,1,0:T(8,128)} %refs_2_.1), custom_call_target="tpu_custom_call" | custom-call | tf_op jit(solution)/shard_map/two_grid/pallas_call | solution.py:450
  68.5 3.4 %store.1 = f32[64,128,256]{2,1,0:T(8,128)} custom-call(f32[2,64,128,128]{3,2,1,0:T(8,128)S(1)} %two_grid.1.held), custom_call_target="tpu_custom_call" | custom-call | tf_op jit(solution)/shard_map/store/pallas_call | solution.py:472

commit v3 on v2

--- a/solution.py
+++ b/solution.py
@@ -37,24 +37,29 @@
     def device(dy, dx):
         return (lax.rem(my + dy + ny, ny), lax.rem(mx + dx + nx, nx))
 
-    def loads(array, ref, padded, spans, base):
+    def loads(array, ref, padded, spans, base, x=0, w=X):
         made = []
         for low, count in spans:
             for j in range(J):
                 if padded:
-                    dst = ref.at[j, pl.ds(1 + low, count), pl.ds(PX, X), :]
+                    dst = ref.at[j, pl.ds(1 + low, count), pl.ds(PX + x, w), :]
                 else:
                     dst = ref.at[j, pl.ds(low, count), :, :]
                 made.append(pltpu.make_async_copy(
-                    array.at[pl.ds(low, count), :, pl.ds(j * 128, 128)], dst, ld_sem.at[base + len(made)]))
+                    array.at[pl.ds(low, count), pl.ds(x, w), pl.ds(j * 128, 128)], dst, ld_sem.at[base + len(made)]))
         return made
 
     quarters = [(n * Y // 4, Y // 4) for n in range(4)]
-    load_ends = loads(initial, U, True, [(0, 1), (Y - 1, 1)], 0)
-    load_u = loads(initial, U, True, [(1, 15), (16, 16), (32, 16), (48, Y - 49)], 2 * J)
-    load_d = loads(absorb, D, False, quarters, 6 * J)
-    load_s = loads(source, S, False, quarters, 10 * J)
-    for copy in load_ends + load_u + load_d + load_s:
+    load_ends = loads(initial, U, True, [(0, 1), (Y - 1, 1)], 0, 8, X - 16)
+    load_tiles = [pltpu.make_async_copy(
+        initial.at[:, pl.ds(x, 8), pl.ds(j * 128, 128)], U.at[j, pl.ds(1, Y), pl.ds(PX + x, 8), :],
+        ld_sem.at[16 * J + 2 * j + n]) for j in range(J) for n, x in enumerate((0, X - 8))]
+    load_u = loads(initial, U, True, [(1, 15), (16, 16), (32, 16), (48, Y - 49)], 2 * J, 8, X - 16)
+    load_d = [pltpu.make_async_copy(absorb.at[pl.ds(low, count)], D.at[pl.ds(low, count)], ld_sem.at[6 * J + n])
+              for n, (low, count) in enumerate(quarters)]
+    load_near = loads(source, S, False, [(0, 4), (Y - 4, 4)], 10 * J)
+    load_s = loads(source, S, False, [(4, 12), (16, 16), (32, 16), (48, Y - 52)], 12 * J)
+    for copy in load_ends + load_tiles + load_u + load_near + load_d + load_s:
         copy.start()
 
     around = [(dy, dx) for dy in (-1, 0, 1) for dx in (-1, 0, 1) if (dy, dx) != (0, 0)]
@@ -135,7 +140,7 @@
         return put
 
     def into_result(j, y, x, w, value):
-        D[j, y, pl.ds(x, w), :] = value
+        D[y, pl.ds(x, w), pl.ds(j * 128, 128)] = value
 
     middle_columns = [(x, min(32, X - 8 - x)) for x in range(8, X - 8, 32)]
     edge_columns = [(0, 8), (X - 8, 8)]
@@ -198,15 +203,15 @@
     rows0, rows1, rows2, rows3 = (rows_copies(0, U), rows_copies(1, V), rows_copies(2, U), rows_copies(3, V))
     cols0, cols1, cols2, cols3 = (columns_copies(0), columns_copies(1), columns_copies(2), columns_copies(3))
     with jax.named_scope("wait_ends"):
-        for copy in load_ends:
+        for copy in load_ends + load_tiles:
             copy.wait()
         start(rows0)
+    with jax.named_scope("pack0"):
+        pack(0, U)
+        start(cols0)
     with jax.named_scope("wait_u"):
         for copy in load_u:
             copy.wait()
-    with jax.named_scope("pack0"):
-        pack(0, U)
-        start(cols0)
 
     with jax.named_scope("wait_d"):
         for copy in load_d:
@@ -220,10 +225,10 @@
         for j in range(J):
             total = jnp.zeros((X, 128), jnp.float32)
             for r in range(RATIO):
-                mass = D[j, cy * RATIO + r]
+                mass = D[cy * RATIO + r, :, pl.ds(j * 128, 128)]
                 total = total + mass
                 whole = 4.0 + mass
-                D[j, cy * RATIO + r] = whole
+                D[cy * RATIO + r, :, pl.ds(j * 128, 128)] = whole
                 W[j, cy * RATIO + r] = 0.8 / whole
             T[j, 0] = total
             CW[j, AGAIN + cy, pl.ds(CPX, CX), :] = 0.8 / (4.0 + 0.25 * fold(T.at[:, 0], j))
@@ -232,27 +237,30 @@
         lax.fori_loop(0, CY, weight_row, 0)
         start(mass_near)
 
-    with jax.named_scope("wait_s"):
-        for copy in load_s:
+    with jax.named_scope("wait_x0"):
+        for copy in load_near:
             copy.wait()
-    with jax.named_scope("middle1"):
-        inner(U, into(V), middle_columns)
-    with jax.named_scope("wait_x0"):
         received(cols0)
-    with jax.named_scope("edges1"):
+    with jax.named_scope("unpack0"):
         unpack_columns(0, U)
-        inner(U, into(V), edge_columns)
     with jax.named_scope("wait_y0"):
         received(rows0)
     with jax.named_scope("outer1"):
         unpack_rows(0, U)
         outer(U, into(V))
         start(rows1)
+    with jax.named_scope("wait_s"):
+        for copy in load_s:
+            copy.wait()
+    with jax.named_scope("edges1"):
+        inner(U, into(V), edge_columns)
         pack(1, V)
         start(cols1)
         start(mass_far)
         pack_corners(0, CW, DEPTH)
         start(mass_corners)
+    with jax.named_scope("middle1"):
+        inner(U, into(V), middle_columns)
 
     sent(rows0)
     with jax.named_scope("middle2"):
@@ -276,7 +284,7 @@
             for x, w in columns:
                 total = None
                 for k, old, around in residual_rows(U, j, cy * RATIO, RATIO, x, w):
-                    term = around - D[j, cy * RATIO + k, pl.ds(x, w), :] * old
+                    term = around - D[cy * RATIO + k, pl.ds(x, w), pl.ds(j * 128, 128)] * old
                     total = term if total is None else total + term
                 T[j, cy, pl.ds(x, w), :] = total
 
@@ -323,7 +331,7 @@
 
     def first(y, carry):
         for j in range(J):
-            CA[j, y] = CW[j, y] * CL[j, y]
+            CA[j, y, pl.ds(CPX - 8, CX + 16), :] = CW[j, y, pl.ds(CPX - 8, CX + 16), :] * CL[j, y, pl.ds(CPX - 8, CX + 16), :]
         return carry
 
     def coarse_sweep(old, new, reach):
@@ -384,17 +392,18 @@
             add_row(1 + cy * RATIO + r)
         return carry
 
-    spread(-1)
-    add_row(0)
-    with jax.named_scope("correct"):
-        lax.fori_loop(0, CY, correct, 0)
+    with jax.named_scope("correct_outer"):
+        spread(-1)
+        add_row(0)
         spread(CY)
         add_row(Y + 1)
-
+        lax.fori_loop(0, 2, lambda i, carry: correct(i * (CY - 1), carry), 0)
     sent(rows1)
     with jax.named_scope("outer3"):
         outer(U, into(V))
         start(rows3)
+    with jax.named_scope("correct"):
+        lax.fori_loop(1, CY - 1, correct, 0)
     with jax.named_scope("sweep3"):
         inner(U, into(V), edge_columns)
         pack(3, V)
@@ -419,12 +428,9 @@
 
 
 def store(held, out, sems):
-    J, Y, X = held.shape[0], held.shape[1], held.shape[2]
-    copies = []
-    for n in range(4):
-        for j in range(J):
-            rows = pl.ds(n * Y // 4, Y // 4)
-            copies.append(pltpu.make_async_copy(held.at[j, rows], out.at[rows, :, pl.ds(j * 128, 128)], sems.at[n, j]))
+    pieces = sems.shape[0]
+    rows = held.shape[0] // pieces
+    copies = [pltpu.make_async_copy(held.at[pl.ds(n * rows, rows)], out.at[pl.ds(n * rows, rows)], sems.at[n]) for n in range(pieces)]
     for copy in copies:
         copy.start()
     for copy in copies:
@@ -449,7 +455,7 @@
 
         held = pl.pallas_call(
             body,
-            out_shape=plain,
+            out_shape=pltpu.VMEM((Y, X, cases), f32),
             in_specs=[pl.BlockSpec(memory_space=pl.ANY)] * 3,
             out_specs=pl.BlockSpec(memory_space=pltpu.VMEM),
             scratch_shapes=[
@@ -461,7 +467,7 @@
                 pltpu.VMEM((4, 2, J, Y, 128), f32),
                 pltpu.VMEM((3, 4, J, 24, 128), f32),
                 pltpu.VMEM((3, 4, J, 24, 128), f32),
-                dma((14 * J,)),
+                dma((18 * J,)),
                 dma((4, 2)), dma((4, 2)), dma((4, 2)), dma((4, 2)),
                 dma((28,)), dma((28,)),
             ],
@@ -474,7 +480,7 @@
             out_shape=jax.ShapeDtypeStruct((Y, X, cases), f32),
             in_specs=[pl.BlockSpec(memory_space=pltpu.VMEM)],
             out_specs=pl.BlockSpec(memory_space=pl.ANY),
-            scratch_shapes=[dma((4, J))],
+            scratch_shapes=[dma((8,))],
             compiler_params=pltpu.CompilerParams(vmem_limit_bytes=1024 * 1024),
             name="store",
         )(pltpu.with_memory_space_constraint(held, pltpu.VMEM))

time: 72 us -> 71 us (0.986)
  Pallas kernels: 71.9 us -> 70.9 us
    pallas_call x1, Pallas kernels: 68.5 us -> 67.6 us  [local(): pl.pallas_call(body, out_shape=pltpu.VMEM((Y, X, cases), f32), in_specs=[...]
where the time goes in v3:
time: 71 us; the launch traced here: 70.9 us
  Pallas kernels  70.9 us (100%)
    pallas_call x1, Pallas kernels, local(): pl.pallas_call(body, out_shape=pltpu.VMEM((Y, X, cases), f32), in_specs=[...  67.6 us
    pallas_call x1, Pallas kernels, local(): pl.pallas_call(store, out_shape=jax.ShapeDtypeStruct((Y, X, cases), f32),...  3.37 us

profile of v3, /device:TPU:1, one launch (start us, length us, event | category | flops | bytes accessed | tf_op | source)
XLA Modules:
  0.0 70.9 jit_solution(7467630625835050125)
XLA Ops:
  0.0 67.6 %two_grid.1.held = f32[64,128,256]{2,1,0:T(8,128)S(1)} custom-call(f32[64,128,256]{2,1,0:T(8,128)} %refs_0_.1, f32[64,128,256]{2,1,0:T(8,128)} %refs_1_.1, f32[64,128,256]{2,1,0:T(8,128)} %refs_2_.1), custom_call_target="tpu_custom_call" | custom-call | tf_op jit(solution)/shard_map/two_grid/pallas_call | solution.py:456
  67.6 3.4 %store.1 = f32[64,128,256]{2,1,0:T(8,128)} custom-call(f32[64,128,256]{2,1,0:T(8,128)S(1)} %two_grid.1.held), custom_call_target="tpu_custom_call" | custom-call | tf_op jit(solution)/shard_map/store/pallas_call | solution.py:478

commit v4 on v3

--- a/solution.py
+++ b/solution.py
@@ -158,6 +158,14 @@
             return carry
         lax.fori_loop(0, 2, body, 0)
 
+    def each_end(k, coming, src, dst, going):
+        for n, low, halo in ((0, 0, 0), (1, Y - 2, Y + 1)):
+            coming[1 - n].wait_recv()
+            for j in range(J):
+                src[j, halo, pl.ds(PX, X), :] = LY[k, n, j]
+            relax(src, into(dst), low, 2, all_columns)
+            going[n].start()
+
     def coarse_copies(ref, pieces, base):
         made = []
         for n, (dy, dx, r, nr, c, nc) in enumerate(pieces):
@@ -243,12 +251,8 @@
         received(cols0)
     with jax.named_scope("unpack0"):
         unpack_columns(0, U)
-    with jax.named_scope("wait_y0"):
-        received(rows0)
     with jax.named_scope("outer1"):
-        unpack_rows(0, U)
-        outer(U, into(V))
-        start(rows1)
+        each_end(0, rows0, U, V, rows1)
     with jax.named_scope("wait_s"):
         for copy in load_s:
             copy.wait()
@@ -270,12 +274,8 @@
     with jax.named_scope("edges2"):
         unpack_columns(1, V)
         inner(V, into(U), edge_columns)
-    with jax.named_scope("wait_y1"):
-        received(rows1)
     with jax.named_scope("outer2"):
-        unpack_rows(1, V)
-        outer(V, into(U))
-        start(rows2)
+        each_end(1, rows1, V, U, rows2)
         pack(2, U)
         start(cols2)
 
@@ -400,8 +400,9 @@
         lax.fori_loop(0, 2, lambda i, carry: correct(i * (CY - 1), carry), 0)
     sent(rows1)
     with jax.named_scope("outer3"):
-        outer(U, into(V))
-        start(rows3)
+        for copy, y in zip(rows3, (0, Y - 2)):
+            relax(U, into(V), y, 2, all_columns)
+            copy.start()
     with jax.named_scope("correct"):
         lax.fori_loop(1, CY - 1, correct, 0)
     with jax.named_scope("sweep3"):

time: 71 us -> 70.9 us (level)
  no operation moved by 1% of the time
where the time goes in v4:
time: 70.9 us; the launch traced here: 70.8 us
  Pallas kernels  70.8 us (100%)
    pallas_call x1, Pallas kernels, local(): pl.pallas_call(body, out_shape=pltpu.VMEM((Y, X, cases), f32), in_specs=[...  67.5 us
    pallas_call x1, Pallas kernels, local(): pl.pallas_call(store, out_shape=jax.ShapeDtypeStruct((Y, X, cases), f32),...  3.37 us

profile of v4, /device:TPU:1, one launch (start us, length us, event | category | flops | bytes accessed | tf_op | source)
XLA Modules:
  0.0 70.8 jit_solution(8542678843391560787)
XLA Ops:
  0.0 67.5 %two_grid.1.held = f32[64,128,256]{2,1,0:T(8,128)S(1)} custom-call(f32[64,128,256]{2,1,0:T(8,128)} %refs_0_.1, f32[64,128,256]{2,1,0:T(8,128)} %refs_1_.1, f32[64,128,256]{2,1,0:T(8,128)} %refs_2_.1), custom_call_target="tpu_custom_call" | custom-call | tf_op jit(solution)/shard_map/two_grid/pallas_call | solution.py:457
  67.5 3.4 %store.1 = f32[64,128,256]{2,1,0:T(8,128)} custom-call(f32[64,128,256]{2,1,0:T(8,128)S(1)} %two_grid.1.held), custom_call_target="tpu_custom_call" | custom-call | tf_op jit(solution)/shard_map/store/pallas_call | solution.py:479
